TPU v7x, 256 devices: a whole 4x4x8 slice. The times are simulated.
256 devices in a mesh: row: 16 (over y_hi, x, core), col: 16 (over z, y_lo).
Axes of the slice: x: 4, y: 4 (y_hi: 2, y_lo: 2; y = y_hi * 2 + y_lo), z: 8, core: 2. Of those that a mesh axis runs over, the one named last changes fastest.
Arguments:
- blocks: bfloat16 [16, 16, 368, 128, 128], P('row', 'col'), may hold values from -0.125 to 0.125
- block_rows: int32 [16, 16, 368], P('row', 'col'), may hold values from 0 to 127, as said below
- block_cols: int32 [16, 16, 368], P('row', 'col'), may hold values from 0 to 127
- counts: int32 [16, 16], P('row', 'col'), may hold values from 1 to 368, as said below
- features: bfloat16 [262144, 256], P(('col', 'row')), may hold values from -6 to 6
Outputs:
- aggregated: bfloat16 [262144, 256], P(('row', 'col'))
Inputs may be any that keep to these rules, and one draw needn't show every extreme that they name: `block_rows`: within one tile the live slots name distinct pairs of block row and block column. `counts`: some tile holds exactly 368 live blocks in every draw.
All inputs are finite; a program needn't handle non-finite values.
Results may differ from a plain program's by a relative error of at most 0.013.
Values may be sent and summed in bfloat16 or wider, within the bound.
No kernel may reach another device: no remote copies, remote signals or barrier semaphores. Data moves between devices by JAX's collectives and lax.ppermute only.
A program may use at most 128 MiB of HBM per device.

v0:
```python
import jax
import jax.numpy as jnp
from jax import lax
from jax.sharding import Mesh
from jax.sharding import PartitionSpec as P

COL = ("col_0", "col_1")
COL_ROW = ("col_0", "col_1", "row")
ROW_COL = ("row", "col_0", "col_1")


def sum_by_axis(array, axes, dim):
    if not axes:
        return array
    nearer = lax.psum_scatter(array, axes[0], scatter_dimension=dim, tiled=True)
    return sum_by_axis(nearer, axes[1:], dim)


def on_device(blocks, block_rows, block_cols, counts, features):
    feature_width = features.shape[1]
    block_size = blocks.shape[-1]
    max_blocks = blocks.shape[2]
    group_size = max_blocks // 8
    row_blocks = lax.axis_size(COL) * (features.shape[0] // block_size)
    panel_rows = lax.all_gather(features, "row", axis=0, tiled=True)
    panel_blocks = panel_rows.reshape(-1, block_size, feature_width)
    tile_blocks = blocks[0, 0]
    tile_rows = block_rows[0, 0]
    tile_cols = block_cols[0, 0]
    live_count = counts[0, 0]

    def accumulate(group_index, running):
        first_slot = group_index * group_size
        weights = lax.dynamic_slice_in_dim(tile_blocks, first_slot, group_size, 0)
        rows_slice = lax.dynamic_slice_in_dim(tile_rows, first_slot, group_size, 0)
        cols_slice = lax.dynamic_slice_in_dim(tile_cols, first_slot, group_size, 0)
        positions = first_slot + jnp.arange(group_size, dtype=jnp.int32)
        weights = jnp.where(
            (positions < live_count)[:, None, None], weights, jnp.zeros_like(weights)
        )
        gathered = panel_blocks[cols_slice, :, 0:feature_width]
        product = jnp.einsum("gik,gkf->gif", weights, gathered, preferred_element_type=jnp.float32)
        return running.at[rows_slice].add(product)

    initial = jnp.zeros((row_blocks, block_size, feature_width - 0), jnp.float32)
    groups = 8
    running = lax.fori_loop(0, groups, accumulate, initial)
    summed = sum_by_axis(
        running.reshape(row_blocks * block_size, feature_width - 0).astype(jnp.bfloat16), COL, 0
    ).astype(jnp.float32)
    return summed.astype(jnp.bfloat16)


def solution(mesh):
    finer = Mesh(mesh.devices.reshape(mesh.shape["row"], 8, 2), ("row", "col_0", "col_1"))
    placed = (
        P("row", COL, None, None, None),
        P("row", COL, None),
        P("row", COL, None),
        P("row", COL),
        P(COL_ROW, None),
    )
    return jax.shard_map(
        on_device, mesh=finer, in_specs=placed, out_specs=P(ROW_COL, None), check_vma=False
    )
```

profile of v0, /device:TPU:1, one launch (start us, length us, event | category | flops | bytes accessed | tf_op | source)
XLA Modules:
  0.0 431.7 jit_solution(5214397716992773565)
XLA Ops:
  6.5 0.7 all-gather.2.cloned.1.call-update
  7.3 0.7 reduce
  8.7 83.5 %all-gather.2.cloned.1.call-done = bf16[16384,256]{1,0:T(8,128)(2,1)} async-done(((bf16[1024,256]{1,0:T(8,128)(2,1)}), bf16[16384,256]{1,0:T(8,128)(2,1)}) %all-gather.2.cloned.1.call-update) | async-done | bytes 8388624 | tf_op jit(solution)/shard_map/all_gather | solution.py:25
  92.2 7.8 %broadcast_in_dim.38 = f32[128,128,256]{2,1,0:T(8,128)} broadcast(f32[]{:T(128)} %constant.44.clone.1), dimensions={} | broadcast | bytes 16777220 | tf_op jit(solution)/shard_map/broadcast_in_dim | solution.py:45
  100.0 196.8 %while.13 = (s32[]{:T(128)}, f32[128,128,256]{2,1,0:T(8,128)}, s32[368]{0:T(512)S(1)}, s32[]{:T(128)}, bf16[368,128,128]{2,1,0:T(8,128)(2,1)}, /*index=5*/s32[36...) while((s32[]{:T(128)}, f32[128,128,256]{2,1,0:T(8,128)}, ...), condition=%wide.region_2.3_spmd, body=%wide.region_0.2_spmd.sunk | while | flops 388138368 | bytes 34674192 | solution.py:47
  100.7 4.1 gather_fusion
  104.9 5.0 %fusion.13 = f32[46,128,256]{2,1,0:T(8,128)} fusion(bf16[46,128,256]{2,1,0:T(8,128)(2,1)S(1)} %gather_fusion, bf16[368,128,128]{2,1,0:T(8,128)(2,1)} %get-tuple-element.219, s32[]{:T(128)S(6)} %select_n.40, pred[46]{0:T(512)(128)(4,1)S(1)} %add_compare_fusion.2), kind=kOutput, calls=%fused_computation.2.clone.1 | convolution fusion | flops 386629632 | bytes 10551346 | tf_op jit(solution)/shard_map/while/body/eval_jaxpr/gik,gkf->gif/dot_general | solution.py:42
  109.9 14.8 %scatter_fusion = f32[128,128,256]{2,1,0:T(8,128)} fusion(f32[128,128,256]{2,1,0:T(8,128)} %get-tuple-element.205, s32[46]{0:T(128)S(1)} %get-tuple-element.191, f32[46,128,256]{2,1,0:T(8,128)} %fusion.13), kind=kCustom, calls=%fused_computation.1.clone.1 | custom fusion | flops 1507328 | bytes 18088120 | tf_op jit(solution)/shard_map/while/body/eval_jaxpr/scatter-add | solution.py:43
  125.4 4.1 gather_fusion
  129.5 5.0 %fusion.13 = f32[46,128,256]{2,1,0:T(8,128)} fusion(bf16[46,128,256]{2,1,0:T(8,128)(2,1)S(1)} %gather_fusion, bf16[368,128,128]{2,1,0:T(8,128)(2,1)} %get-tuple-element.219, s32[]{:T(128)S(6)} %select_n.40, pred[46]{0:T(512)(128)(4,1)S(1)} %add_compare_fusion.2), kind=kOutput, calls=%fused_computation.2.clone.1 | convolution fusion | flops 386629632 | bytes 10551346 | tf_op jit(solution)/shard_map/while/body/eval_jaxpr/gik,gkf->gif/dot_general | solution.py:42
  134.5 14.7 %scatter_fusion = f32[128,128,256]{2,1,0:T(8,128)} fusion(f32[128,128,256]{2,1,0:T(8,128)} %get-tuple-element.205, s32[46]{0:T(128)S(1)} %get-tuple-element.191, f32[46,128,256]{2,1,0:T(8,128)} %fusion.13), kind=kCustom, calls=%fused_computation.1.clone.1 | custom fusion | flops 1507328 | bytes 18088120 | tf_op jit(solution)/shard_map/while/body/eval_jaxpr/scatter-add | solution.py:43
  150.0 4.1 gather_fusion
  154.1 5.0 %fusion.13 = f32[46,128,256]{2,1,0:T(8,128)} fusion(bf16[46,128,256]{2,1,0:T(8,128)(2,1)S(1)} %gather_fusion, bf16[368,128,128]{2,1,0:T(8,128)(2,1)} %get-tuple-element.219, s32[]{:T(128)S(6)} %select_n.40, pred[46]{0:T(512)(128)(4,1)S(1)} %add_compare_fusion.2), kind=kOutput, calls=%fused_computation.2.clone.1 | convolution fusion | flops 386629632 | bytes 10551346 | tf_op jit(solution)/shard_map/while/body/eval_jaxpr/gik,gkf->gif/dot_general | solution.py:42
  159.2 14.7 %scatter_fusion = f32[128,128,256]{2,1,0:T(8,128)} fusion(f32[128,128,256]{2,1,0:T(8,128)} %get-tuple-element.205, s32[46]{0:T(128)S(1)} %get-tuple-element.191, f32[46,128,256]{2,1,0:T(8,128)} %fusion.13), kind=kCustom, calls=%fused_computation.1.clone.1 | custom fusion | flops 1507328 | bytes 18088120 | tf_op jit(solution)/shard_map/while/body/eval_jaxpr/scatter-add | solution.py:43
  174.6 4.1 gather_fusion
  178.7 5.0 %fusion.13 = f32[46,128,256]{2,1,0:T(8,128)} fusion(bf16[46,128,256]{2,1,0:T(8,128)(2,1)S(1)} %gather_fusion, bf16[368,128,128]{2,1,0:T(8,128)(2,1)} %get-tuple-element.219, s32[]{:T(128)S(6)} %select_n.40, pred[46]{0:T(512)(128)(4,1)S(1)} %add_compare_fusion.2), kind=kOutput, calls=%fused_computation.2.clone.1 | convolution fusion | flops 386629632 | bytes 10551346 | tf_op jit(solution)/shard_map/while/body/eval_jaxpr/gik,gkf->gif/dot_general | solution.py:42
  183.7 14.7 %scatter_fusion = f32[128,128,256]{2,1,0:T(8,128)} fusion(f32[128,128,256]{2,1,0:T(8,128)} %get-tuple-element.205, s32[46]{0:T(128)S(1)} %get-tuple-element.191, f32[46,128,256]{2,1,0:T(8,128)} %fusion.13), kind=kCustom, calls=%fused_computation.1.clone.1 | custom fusion | flops 1507328 | bytes 18088120 | tf_op jit(solution)/shard_map/while/body/eval_jaxpr/scatter-add | solution.py:43
  199.2 4.1 gather_fusion
  203.3 5.0 %fusion.13 = f32[46,128,256]{2,1,0:T(8,128)} fusion(bf16[46,128,256]{2,1,0:T(8,128)(2,1)S(1)} %gather_fusion, bf16[368,128,128]{2,1,0:T(8,128)(2,1)} %get-tuple-element.219, s32[]{:T(128)S(6)} %select_n.40, pred[46]{0:T(512)(128)(4,1)S(1)} %add_compare_fusion.2), kind=kOutput, calls=%fused_computation.2.clone.1 | convolution fusion | flops 386629632 | bytes 10551346 | tf_op jit(solution)/shard_map/while/body/eval_jaxpr/gik,gkf->gif/dot_general | solution.py:42
  208.3 14.7 %scatter_fusion = f32[128,128,256]{2,1,0:T(8,128)} fusion(f32[128,128,256]{2,1,0:T(8,128)} %get-tuple-element.205, s32[46]{0:T(128)S(1)} %get-tuple-element.191, f32[46,128,256]{2,1,0:T(8,128)} %fusion.13), kind=kCustom, calls=%fused_computation.1.clone.1 | custom fusion | flops 1507328 | bytes 18088120 | tf_op jit(solution)/shard_map/while/body/eval_jaxpr/scatter-add | solution.py:43
  223.7 4.1 gather_fusion
  227.8 5.0 %fusion.13 = f32[46,128,256]{2,1,0:T(8,128)} fusion(bf16[46,128,256]{2,1,0:T(8,128)(2,1)S(1)} %gather_fusion, bf16[368,128,128]{2,1,0:T(8,128)(2,1)} %get-tuple-element.219, s32[]{:T(128)S(6)} %select_n.40, pred[46]{0:T(512)(128)(4,1)S(1)} %add_compare_fusion.2), kind=kOutput, calls=%fused_computation.2.clone.1 | convolution fusion | flops 386629632 | bytes 10551346 | tf_op jit(solution)/shard_map/while/body/eval_jaxpr/gik,gkf->gif/dot_general | solution.py:42
  232.8 14.7 %scatter_fusion = f32[128,128,256]{2,1,0:T(8,128)} fusion(f32[128,128,256]{2,1,0:T(8,128)} %get-tuple-element.205, s32[46]{0:T(128)S(1)} %get-tuple-element.191, f32[46,128,256]{2,1,0:T(8,128)} %fusion.13), kind=kCustom, calls=%fused_computation.1.clone.1 | custom fusion | flops 1507328 | bytes 18088120 | tf_op jit(solution)/shard_map/while/body/eval_jaxpr/scatter-add | solution.py:43
  248.3 4.1 gather_fusion
  252.4 5.0 %fusion.13 = f32[46,128,256]{2,1,0:T(8,128)} fusion(bf16[46,128,256]{2,1,0:T(8,128)(2,1)S(1)} %gather_fusion, bf16[368,128,128]{2,1,0:T(8,128)(2,1)} %get-tuple-element.219, s32[]{:T(128)S(6)} %select_n.40, pred[46]{0:T(512)(128)(4,1)S(1)} %add_compare_fusion.2), kind=kOutput, calls=%fused_computation.2.clone.1 | convolution fusion | flops 386629632 | bytes 10551346 | tf_op jit(solution)/shard_map/while/body/eval_jaxpr/gik,gkf->gif/dot_general | solution.py:42
  257.4 14.7 %scatter_fusion = f32[128,128,256]{2,1,0:T(8,128)} fusion(f32[128,128,256]{2,1,0:T(8,128)} %get-tuple-element.205, s32[46]{0:T(128)S(1)} %get-tuple-element.191, f32[46,128,256]{2,1,0:T(8,128)} %fusion.13), kind=kCustom, calls=%fused_computation.1.clone.1 | custom fusion | flops 1507328 | bytes 18088120 | tf_op jit(solution)/shard_map/while/body/eval_jaxpr/scatter-add | solution.py:43
  272.9 4.1 gather_fusion
  277.0 5.0 %fusion.13 = f32[46,128,256]{2,1,0:T(8,128)} fusion(bf16[46,128,256]{2,1,0:T(8,128)(2,1)S(1)} %gather_fusion, bf16[368,128,128]{2,1,0:T(8,128)(2,1)} %get-tuple-element.219, s32[]{:T(128)S(6)} %select_n.40, pred[46]{0:T(512)(128)(4,1)S(1)} %add_compare_fusion.2), kind=kOutput, calls=%fused_computation.2.clone.1 | convolution fusion | flops 386629632 | bytes 10551346 | tf_op jit(solution)/shard_map/while/body/eval_jaxpr/gik,gkf->gif/dot_general | solution.py:42
  282.0 14.8 %scatter_fusion = f32[128,128,256]{2,1,0:T(8,128)} fusion(f32[128,128,256]{2,1,0:T(8,128)} %get-tuple-element.205, s32[46]{0:T(128)S(1)} %get-tuple-element.191, f32[46,128,256]{2,1,0:T(8,128)} %fusion.13), kind=kCustom, calls=%fused_computation.1.clone.1 | custom fusion | flops 1507328 | bytes 18088120 | tf_op jit(solution)/shard_map/while/body/eval_jaxpr/scatter-add | solution.py:43
  296.8 9.0 %convert_element_type.8 = bf16[128,128,256]{2,1,0:T(8,128)(2,1)} convert(f32[128,128,256]{2,1,0:T(8,128)} %get-tuple-element.129) | non-fusion elementwise | flops 4194304 | bytes 25165824 | tf_op jit(solution)/shard_map/convert_element_type | solution.py:49
  305.9 92.8 %reduce-scatter.3.cloned.1.call-done = bf16[2048,256]{1,0:T(8,128)(2,1)} async-done(((bf16[16384,256]{1,0:T(8,128)(2,1)}), bf16[2048,256]{1,0:T(8,128)(2,1)}) %reduce-scatter.3.cloned.1.call-update) | async-done | bytes 1048592 | tf_op jit(solution)/shard_map/reduce_scatter | solution.py:15
  398.7 26.5 %reduce-scatter.5.cloned.1.call-done = bf16[1024,256]{1,0:T(8,128)(2,1)} async-done(((bf16[2048,256]{1,0:T(8,128)(2,1)}), bf16[1024,256]{1,0:T(8,128)(2,1)}) %reduce-scatter.5.cloned.1.call-update) | async-done | bytes 524304 | tf_op jit(solution)/shard_map/reduce_scatter | solution.py:15
  (30 shorter events, 6.7 us)
Async XLA Ops:
  6.5 85.6 %all-gather.2.cloned.1.call-start = ((), (), s32[]{:S(2)}) async-start(), calls=%async_computation.2 | async-start | bytes 8912896 | tf_op jit(solution)/shard_map/all_gather | solution.py:25
  7.3 391.4 %reduce-scatter.3.cloned.1.call-start = ((), (), s32[]{:S(2)}) async-start(), calls=%async_computation.3 | async-start | bytes 9437184 | tf_op jit(solution)/shard_map/reduce_scatter | solution.py:15
  305.8 119.3 %reduce-scatter.5.cloned.1.call-start = ((), (), s32[]{:S(2)}) async-start(), calls=%async_computation.4 | async-start | bytes 1572864 | tf_op jit(solution)/shard_map/reduce_scatter | solution.py:15
Sparse Core Ops, SparseCore 0:
  10.1 82.0 all-gather.1
  305.9 92.6 reduce-scatter.2
  401.1 23.9 reduce-scatter.4
where the time goes:
time: 433 us; the launch traced here: 432 us
  waiting for transfers between devices  203 us (47%)
  other arithmetic  134 us (31%)
  local copies, waits for them, and re-layouts  40.8 us (9%)
  matrix products  40.1 us (9%)
  between operations  13.1 us (3%)
    reduce_scatter x2, waiting for transfers between devices, sum_by_axis(): nearer = lax.psum_scatter(array, axes[0], scatter_dimension=dim, tiled=True)  119 us
    scatter-add x8, other arithmetic, accumulate(): return running.at[rows_slice].add(product)  118 us
    all_gather x1, waiting for transfers between devices, on_device(): panel_rows = lax.all_gather(features, 'row', axis=0, tiled=True)  83.5 us
    dot_general x8, matrix products, accumulate(): jnp.einsum('gik,gkf->gif', weights, gathered, preferred_element_type=jnp....  40.1 us
    gather x8, local copies, waits for them, and re-layouts, accumulate(): gathered = panel_blocks[cols_slice, :, 0:feature_width]  33 us
    convert_element_type x1, other arithmetic, on_device(): running.reshape(row_blocks * block_size, feature_width - 0)  9.02 us
  transfers between devices with their start and end apart: 3, of which 3 were waited for; matrix products, arithmetic and copies ran while one was open for 0% of the time, Pallas kernels for 0%

commit v1 on v0

--- a/solution.py
+++ b/solution.py
@@ -22,7 +22,9 @@
     max_blocks = blocks.shape[2]
     group_size = max_blocks // 8
     row_blocks = lax.axis_size(COL) * (features.shape[0] // block_size)
-    panel_rows = lax.all_gather(features, "row", axis=0, tiled=True)
+    panel_rows = jnp.concatenate(
+        lax.all_to_all(jnp.stack([features for _ in range(lax.psum(1, "row"))]), "row", 0, 0), 0
+    )
     panel_blocks = panel_rows.reshape(-1, block_size, feature_width)
     tile_blocks = blocks[0, 0]
     tile_rows = block_rows[0, 0]

time: 433 us -> 478 us (1.10)
  waiting for transfers between devices: 203 us -> 236 us
  starting transfers between devices: 0.08 us -> 8.64 us
  local copies, waits for them, and re-layouts: 40.8 us -> 45.9 us
    all_to_all x0 -> x1, waiting for transfers between devices: none -> 112 us  [on_device(): lax.all_to_all(jnp.stack([features for _ in range(lax.psum(1, 'row'))]),...]
    all_gather x1 -> x0, waiting for transfers between devices: 83.5 us -> none  [on_device(): panel_rows = lax.all_gather(features, 'row', axis=0, tiled=True)]
    all_to_all x0 -> x1, starting transfers between devices: none -> 8.57 us  [on_device(): lax.all_to_all(jnp.stack([features for _ in range(lax.psum(1, 'row'))]),...]
    another operation x0 -> x1, local copies, waits for them, and re-layouts: none -> 5.07 us  [on_device(): jnp.stack([features for _ in range(lax.psum(1, 'row'))])]
where the time goes in v1:
time: 478 us; the launch traced here: 477 us
  waiting for transfers between devices  236 us (49%)
  other arithmetic  133 us (28%)
  local copies, waits for them, and re-layouts  45.9 us (10%)
  matrix products  40.1 us (8%)
  between operations  13.4 us (3%)
  starting transfers between devices  8.64 us (2%)
    reduce_scatter x2, waiting for transfers between devices, sum_by_axis(): nearer = lax.psum_scatter(array, axes[0], scatter_dimension=dim, tiled=True)  123 us
    scatter-add x8, other arithmetic, accumulate(): return running.at[rows_slice].add(product)  118 us
    all_to_all x1, waiting for transfers between devices, on_device(): lax.all_to_all(jnp.stack([features for _ in range(lax.psum(1, 'row'))]),...  112 us
    dot_general x8, matrix products, accumulate(): jnp.einsum('gik,gkf->gif', weights, gathered, preferred_element_type=jnp....  40.1 us
    gather x8, local copies, waits for them, and re-layouts, accumulate(): gathered = panel_blocks[cols_slice, :, 0:feature_width]  33 us
  transfers between devices with their start and end apart: 3, of which 3 were waited for; matrix products, arithmetic and copies ran while one was open for 0% of the time, Pallas kernels for 0%

profile of v1, /device:TPU:1, one launch (start us, length us, event | category | flops | bytes accessed | tf_op | source)
XLA Modules:
  0.0 476.6 jit_solution(15375631132397673037)
XLA Ops:
  6.5 5.1 %stack.2 = bf16[16,1024,256]{2,1,0:T(8,128)(2,1)} broadcast(bf16[1024,256]{1,0:T(8,128)(2,1)} %param.11), dimensions={1,2} | broadcast | bytes 8912896 | tf_op jit(solution)/shard_map/stack | solution.py:26
  11.6 8.6 %all-to-all-start = ((bf16[16,1024,256]{2,1,0:T(8,128)(2,1)}), bf16[16,1024,256]{2,1,0:T(8,128)(2,1)}, u32[]{:S(2)}, u32[]{:S(2)}) async-start(bf16[16,1024,256]{2,1,0:T(8,128)(2,1)} %stack.2), calls=%async_computation | async-start | bytes 16777216 | tf_op jit(solution)/shard_map/all_to_all | solution.py:26
  20.3 112.4 %all-to-all-done = bf16[16,1024,256]{2,1,0:T(8,128)(2,1)} async-done(((bf16[16,1024,256]{2,1,0:T(8,128)(2,1)}), bf16[16,1024,256]{2,1,0:T(8,128)(2,1)}, u32[]{:S(2)}, u32[]{:S(2)}) %all-to-all-start) | async-done | bytes 8388640 | tf_op jit(solution)/shard_map/all_to_all | solution.py:26
  132.6 7.8 %broadcast_in_dim.38 = f32[128,128,256]{2,1,0:T(8,128)} broadcast(f32[]{:T(128)} %constant.44.clone.1), dimensions={} | broadcast | bytes 16777220 | tf_op jit(solution)/shard_map/broadcast_in_dim | solution.py:47
  140.5 196.8 %while.13 = (s32[]{:T(128)}, f32[128,128,256]{2,1,0:T(8,128)}, s32[368]{0:T(512)S(1)}, s32[]{:T(128)}, bf16[368,128,128]{2,1,0:T(8,128)(2,1)}, /*index=5*/s32[36...) while((s32[]{:T(128)}, f32[128,128,256]{2,1,0:T(8,128)}, ...), condition=%wide.region_2.3_spmd, body=%wide.region_0.2_spmd.sunk | while | flops 388138368 | bytes 34674192 | solution.py:49
  141.2 4.1 gather_fusion
  145.3 5.0 %fusion.13 = f32[46,128,256]{2,1,0:T(8,128)} fusion(bf16[46,128,256]{2,1,0:T(8,128)(2,1)S(1)} %gather_fusion, bf16[368,128,128]{2,1,0:T(8,128)(2,1)} %get-tuple-element.219, s32[]{:T(128)S(6)} %select_n.40, pred[46]{0:T(512)(128)(4,1)S(1)} %add_compare_fusion.2), kind=kOutput, calls=%fused_computation.2.clone.1 | convolution fusion | flops 386629632 | bytes 10551346 | tf_op jit(solution)/shard_map/while/body/eval_jaxpr/gik,gkf->gif/dot_general | solution.py:44
  150.3 14.8 %scatter_fusion = f32[128,128,256]{2,1,0:T(8,128)} fusion(f32[128,128,256]{2,1,0:T(8,128)} %get-tuple-element.205, s32[46]{0:T(128)S(1)} %get-tuple-element.191, f32[46,128,256]{2,1,0:T(8,128)} %fusion.13), kind=kCustom, calls=%fused_computation.1.clone.1 | custom fusion | flops 1507328 | bytes 18088120 | tf_op jit(solution)/shard_map/while/body/eval_jaxpr/scatter-add | solution.py:45
  165.9 4.1 gather_fusion
  170.0 5.0 %fusion.13 = f32[46,128,256]{2,1,0:T(8,128)} fusion(bf16[46,128,256]{2,1,0:T(8,128)(2,1)S(1)} %gather_fusion, bf16[368,128,128]{2,1,0:T(8,128)(2,1)} %get-tuple-element.219, s32[]{:T(128)S(6)} %select_n.40, pred[46]{0:T(512)(128)(4,1)S(1)} %add_compare_fusion.2), kind=kOutput, calls=%fused_computation.2.clone.1 | convolution fusion | flops 386629632 | bytes 10551346 | tf_op jit(solution)/shard_map/while/body/eval_jaxpr/gik,gkf->gif/dot_general | solution.py:44
  175.0 14.7 %scatter_fusion = f32[128,128,256]{2,1,0:T(8,128)} fusion(f32[128,128,256]{2,1,0:T(8,128)} %get-tuple-element.205, s32[46]{0:T(128)S(1)} %get-tuple-element.191, f32[46,128,256]{2,1,0:T(8,128)} %fusion.13), kind=kCustom, calls=%fused_computation.1.clone.1 | custom fusion | flops 1507328 | bytes 18088120 | tf_op jit(solution)/shard_map/while/body/eval_jaxpr/scatter-add | solution.py:45
  190.5 4.1 gather_fusion
  194.6 5.0 %fusion.13 = f32[46,128,256]{2,1,0:T(8,128)} fusion(bf16[46,128,256]{2,1,0:T(8,128)(2,1)S(1)} %gather_fusion, bf16[368,128,128]{2,1,0:T(8,128)(2,1)} %get-tuple-element.219, s32[]{:T(128)S(6)} %select_n.40, pred[46]{0:T(512)(128)(4,1)S(1)} %add_compare_fusion.2), kind=kOutput, calls=%fused_computation.2.clone.1 | convolution fusion | flops 386629632 | bytes 10551346 | tf_op jit(solution)/shard_map/while/body/eval_jaxpr/gik,gkf->gif/dot_general | solution.py:44
  199.6 14.7 %scatter_fusion = f32[128,128,256]{2,1,0:T(8,128)} fusion(f32[128,128,256]{2,1,0:T(8,128)} %get-tuple-element.205, s32[46]{0:T(128)S(1)} %get-tuple-element.191, f32[46,128,256]{2,1,0:T(8,128)} %fusion.13), kind=kCustom, calls=%fused_computation.1.clone.1 | custom fusion | flops 1507328 | bytes 18088120 | tf_op jit(solution)/shard_map/while/body/eval_jaxpr/scatter-add | solution.py:45
  215.0 4.1 gather_fusion
  219.2 5.0 %fusion.13 = f32[46,128,256]{2,1,0:T(8,128)} fusion(bf16[46,128,256]{2,1,0:T(8,128)(2,1)S(1)} %gather_fusion, bf16[368,128,128]{2,1,0:T(8,128)(2,1)} %get-tuple-element.219, s32[]{:T(128)S(6)} %select_n.40, pred[46]{0:T(512)(128)(4,1)S(1)} %add_compare_fusion.2), kind=kOutput, calls=%fused_computation.2.clone.1 | convolution fusion | flops 386629632 | bytes 10551346 | tf_op jit(solution)/shard_map/while/body/eval_jaxpr/gik,gkf->gif/dot_general | solution.py:44
  224.2 14.7 %scatter_fusion = f32[128,128,256]{2,1,0:T(8,128)} fusion(f32[128,128,256]{2,1,0:T(8,128)} %get-tuple-element.205, s32[46]{0:T(128)S(1)} %get-tuple-element.191, f32[46,128,256]{2,1,0:T(8,128)} %fusion.13), kind=kCustom, calls=%fused_computation.1.clone.1 | custom fusion | flops 1507328 | bytes 18088120 | tf_op jit(solution)/shard_map/while/body/eval_jaxpr/scatter-add | solution.py:45
  239.6 4.1 gather_fusion
  243.8 5.0 %fusion.13 = f32[46,128,256]{2,1,0:T(8,128)} fusion(bf16[46,128,256]{2,1,0:T(8,128)(2,1)S(1)} %gather_fusion, bf16[368,128,128]{2,1,0:T(8,128)(2,1)} %get-tuple-element.219, s32[]{:T(128)S(6)} %select_n.40, pred[46]{0:T(512)(128)(4,1)S(1)} %add_compare_fusion.2), kind=kOutput, calls=%fused_computation.2.clone.1 | convolution fusion | flops 386629632 | bytes 10551346 | tf_op jit(solution)/shard_map/while/body/eval_jaxpr/gik,gkf->gif/dot_general | solution.py:44
  248.8 14.7 %scatter_fusion = f32[128,128,256]{2,1,0:T(8,128)} fusion(f32[128,128,256]{2,1,0:T(8,128)} %get-tuple-element.205, s32[46]{0:T(128)S(1)} %get-tuple-element.191, f32[46,128,256]{2,1,0:T(8,128)} %fusion.13), kind=kCustom, calls=%fused_computation.1.clone.1 | custom fusion | flops 1507328 | bytes 18088120 | tf_op jit(solution)/shard_map/while/body/eval_jaxpr/scatter-add | solution.py:45
  264.2 4.1 gather_fusion
  268.3 5.0 %fusion.13 = f32[46,128,256]{2,1,0:T(8,128)} fusion(bf16[46,128,256]{2,1,0:T(8,128)(2,1)S(1)} %gather_fusion, bf16[368,128,128]{2,1,0:T(8,128)(2,1)} %get-tuple-element.219, s32[]{:T(128)S(6)} %select_n.40, pred[46]{0:T(512)(128)(4,1)S(1)} %add_compare_fusion.2), kind=kOutput, calls=%fused_computation.2.clone.1 | convolution fusion | flops 386629632 | bytes 10551346 | tf_op jit(solution)/shard_map/while/body/eval_jaxpr/gik,gkf->gif/dot_general | solution.py:44
  273.3 14.7 %scatter_fusion = f32[128,128,256]{2,1,0:T(8,128)} fusion(f32[128,128,256]{2,1,0:T(8,128)} %get-tuple-element.205, s32[46]{0:T(128)S(1)} %get-tuple-element.191, f32[46,128,256]{2,1,0:T(8,128)} %fusion.13), kind=kCustom, calls=%fused_computation.1.clone.1 | custom fusion | flops 1507328 | bytes 18088120 | tf_op jit(solution)/shard_map/while/body/eval_jaxpr/scatter-add | solution.py:45
  288.8 4.1 gather_fusion
  292.9 5.0 %fusion.13 = f32[46,128,256]{2,1,0:T(8,128)} fusion(bf16[46,128,256]{2,1,0:T(8,128)(2,1)S(1)} %gather_fusion, bf16[368,128,128]{2,1,0:T(8,128)(2,1)} %get-tuple-element.219, s32[]{:T(128)S(6)} %select_n.40, pred[46]{0:T(512)(128)(4,1)S(1)} %add_compare_fusion.2), kind=kOutput, calls=%fused_computation.2.clone.1 | convolution fusion | flops 386629632 | bytes 10551346 | tf_op jit(solution)/shard_map/while/body/eval_jaxpr/gik,gkf->gif/dot_general | solution.py:44
  297.9 14.7 %scatter_fusion = f32[128,128,256]{2,1,0:T(8,128)} fusion(f32[128,128,256]{2,1,0:T(8,128)} %get-tuple-element.205, s32[46]{0:T(128)S(1)} %get-tuple-element.191, f32[46,128,256]{2,1,0:T(8,128)} %fusion.13), kind=kCustom, calls=%fused_computation.1.clone.1 | custom fusion | flops 1507328 | bytes 18088120 | tf_op jit(solution)/shard_map/while/body/eval_jaxpr/scatter-add | solution.py:45
  313.3 4.1 gather_fusion
  317.5 5.0 %fusion.13 = f32[46,128,256]{2,1,0:T(8,128)} fusion(bf16[46,128,256]{2,1,0:T(8,128)(2,1)S(1)} %gather_fusion, bf16[368,128,128]{2,1,0:T(8,128)(2,1)} %get-tuple-element.219, s32[]{:T(128)S(6)} %select_n.40, pred[46]{0:T(512)(128)(4,1)S(1)} %add_compare_fusion.2), kind=kOutput, calls=%fused_computation.2.clone.1 | convolution fusion | flops 386629632 | bytes 10551346 | tf_op jit(solution)/shard_map/while/body/eval_jaxpr/gik,gkf->gif/dot_general | solution.py:44
  322.5 14.8 %scatter_fusion = f32[128,128,256]{2,1,0:T(8,128)} fusion(f32[128,128,256]{2,1,0:T(8,128)} %get-tuple-element.205, s32[46]{0:T(128)S(1)} %get-tuple-element.191, f32[46,128,256]{2,1,0:T(8,128)} %fusion.13), kind=kCustom, calls=%fused_computation.1.clone.1 | custom fusion | flops 1507328 | bytes 18088120 | tf_op jit(solution)/shard_map/while/body/eval_jaxpr/scatter-add | solution.py:45
  337.3 9.0 %convert_element_type.8 = bf16[128,128,256]{2,1,0:T(8,128)(2,1)} convert(f32[128,128,256]{2,1,0:T(8,128)} %get-tuple-element.129) | non-fusion elementwise | flops 4194304 | bytes 25165824 | tf_op jit(solution)/shard_map/convert_element_type | solution.py:51
  346.3 96.9 %reduce-scatter.3.cloned.1.call-done = bf16[2048,256]{1,0:T(8,128)(2,1)} async-done(((bf16[16384,256]{1,0:T(8,128)(2,1)}), bf16[2048,256]{1,0:T(8,128)(2,1)}) %reduce-scatter.3.cloned.1.call-update) | async-done | bytes 1048592 | tf_op jit(solution)/shard_map/reduce_scatter | solution.py:15
  443.2 26.5 %reduce-scatter.5.cloned.1.call-done = bf16[1024,256]{1,0:T(8,128)(2,1)} async-done(((bf16[2048,256]{1,0:T(8,128)(2,1)}), bf16[1024,256]{1,0:T(8,128)(2,1)}) %reduce-scatter.5.cloned.1.call-update) | async-done | bytes 524304 | tf_op jit(solution)/shard_map/reduce_scatter | solution.py:15
  (34 shorter events, 6.1 us)
Async XLA Ops:
  11.6 8.6 %copy-start = (s32[1,1,368]{2,1,0:T(1,128)S(1)}, s32[1,1,368]{2,1,0:T(1,128)}, u32[]{:S(2)}) copy-start(s32[1,1,368]{2,1,0:T(1,128)} %param.8) | copy-start | bytes 4420
  11.6 8.6 %copy-start.1 = (s32[1,1,368]{2,1,0:T(1,128)S(1)}, s32[1,1,368]{2,1,0:T(1,128)}, u32[]{:S(2)}) copy-start(s32[1,1,368]{2,1,0:T(1,128)} %param.9) | copy-start | bytes 4420
  11.6 121.0 %all-to-all-start = ((bf16[16,1024,256]{2,1,0:T(8,128)(2,1)}), bf16[16,1024,256]{2,1,0:T(8,128)(2,1)}, u32[]{:S(2)}, u32[]{:S(2)}) async-start(bf16[16,1024,256]{2,1,0:T(8,128)(2,1)} %stack.2), calls=%async_computation | async-start | bytes 16777216 | tf_op jit(solution)/shard_map/all_to_all | solution.py:26
  20.2 423.0 %reduce-scatter.3.cloned.1.call-start = ((), (), s32[]{:S(2)}) async-start(), calls=%async_computation.3 | async-start | bytes 9437184 | tf_op jit(solution)/shard_map/reduce_scatter | solution.py:15
  346.3 123.4 %reduce-scatter.5.cloned.1.call-start = ((), (), s32[]{:S(2)}) async-start(), calls=%async_computation.4 | async-start | bytes 1572864 | tf_op jit(solution)/shard_map/reduce_scatter | solution.py:15
Sparse Core Ops, SparseCore 0:
  346.4 96.7 reduce-scatter.2
  445.7 23.9 reduce-scatter.4
